TPU v7x, 64 devices: a 2x2x8 block of a 4x4x8 slice. The times are simulated.
64 devices in a mesh: batch: 4 (over x, y), row: 16 (over z, core).
Axes of the slice: x: 2, y: 2, z: 8, core: 2. Of those that a mesh axis runs over, the one named last changes fastest.
The devices are a block of a 4x4x8 slice.
Arguments:
- trans_mat: bfloat16 [16384, 4096], P(('batch', 'row')), parts along dimension 0
- teleport: float32 [16384, 1024], P(('batch', 'row')), parts along dimension 0
- dangling: int32 [16384], P(('batch', 'row')), parts along dimension 0
- damping: float32 [12], replicated
- rank_init: float32 [16384, 1024], P(('batch', 'row')), parts along dimension 0
Outputs:
- output: float32 [16384, 1024], P(('batch', 'row')), parts along dimension 0
There are 4 independent parts. A program takes and returns all parts, laid end to end along the dimension named above; an argument that names none is the same for every part.
All inputs are finite; a program needn't handle non-finite values.
Results may differ from a plain program's by a relative error of at most 0.001.
Values are sent between devices in bfloat16 or wider.
A program may use at most 768 MiB of HBM per device.

v0:
```python
import jax
import jax.numpy as jnp
from jax import lax
from jax.sharding import PartitionSpec as P, NamedSharding


def solution(mesh):
    spec_rows = P(("batch", "row"), None)
    spec_vec = P(("batch", "row"))

    def local_sweeps(mat_rows, tele_rows, dang_rows, damping, start_rows):
        num_nodes = mat_rows.shape[1]
        dang_float = dang_rows.astype(jnp.float32)
        rank_rows = start_rows
        for sweep_idx in range(damping.shape[0]):
            gathered = lax.all_gather(rank_rows.astype(jnp.bfloat16), "row", axis=0, tiled=True)
            dang_mass = lax.psum(jnp.dot(dang_float, rank_rows, preferred_element_type=jnp.float32), "row")
            prod_rows = jnp.dot(mat_rows, gathered, preferred_element_type=jnp.float32)
            factor = damping[sweep_idx]
            rank_rows = factor * prod_rows + (1.0 - factor) * tele_rows + (factor / num_nodes) * dang_mass[None, :]
        return rank_rows

    sharded_fn = jax.shard_map(local_sweeps, mesh=mesh, in_specs=(spec_rows, spec_rows, spec_vec, P(None), spec_rows), out_specs=spec_rows, check_vma=False)
    return sharded_fn
```

profile of v0, /device:TPU:53, one launch (start us, length us, event | category | flops | bytes accessed | tf_op | source)
XLA Modules:
  0.0 811.7 jit_solution(4615944370918634223)
XLA Ops:
  14.1 25.6 %psum.84 = f32[1024]{0:T(1024)S(1)} all-reduce(f32[1024]{0:T(1024)S(1)} %bitcast.163), channel_id=1, replica_groups=mesh['batch'=4,'row'=16] {'row'}, use_global_device_ids=true, to_apply=%region_0.0 | all-reduce | flops 1024 | bytes 8192 | tf_op jit(solution)/shard_map/psum | solution.py:17
  39.7 24.1 %all-gather.13.cloned.1.call-done = bf16[4096,1024]{1,0:T(8,128)(2,1)} async-done(((bf16[256,1024]{1,0:T(8,128)(2,1)}), bf16[4096,1024]{1,0:T(8,128)(2,1)}) %all-gather.13.cloned.1.call-update) | async-done | bytes 8388624 | tf_op jit(solution)/shard_map/all_gather | solution.py:16
  63.8 7.5 fusion.34
  75.0 23.1 %psum.85 = f32[1024]{0:T(1024)S(1)} all-reduce(f32[1024]{0:T(1024)S(1)} %bitcast.164), channel_id=1, replica_groups=mesh['batch'=4,'row'=16] {'row'}, use_global_device_ids=true, to_apply=%region_1.0 | all-reduce | flops 1024 | bytes 8192 | tf_op jit(solution)/shard_map/psum | solution.py:17
  98.1 24.8 %all-gather.15.cloned.1.call-done = bf16[4096,1024]{1,0:T(8,128)(2,1)} async-done(((bf16[256,1024]{1,0:T(8,128)(2,1)}), bf16[4096,1024]{1,0:T(8,128)(2,1)}) %all-gather.15.cloned.1.call-update) | async-done | bytes 8388624 | tf_op jit(solution)/shard_map/all_gather | solution.py:16
  122.9 7.4 fusion.33
  132.9 22.5 %psum.86 = f32[1024]{0:T(1024)S(1)} all-reduce(f32[1024]{0:T(1024)S(1)} %bitcast.165), channel_id=1, replica_groups=mesh['batch'=4,'row'=16] {'row'}, use_global_device_ids=true, to_apply=%region_2.0 | all-reduce | flops 1024 | bytes 8192 | tf_op jit(solution)/shard_map/psum | solution.py:17
  155.5 35.4 %all-gather.17.cloned.1.call-done = bf16[4096,1024]{0,1:T(8,128)(2,1)} async-done(((bf16[256,1024]{0,1:T(8,128)(2,1)}), bf16[4096,1024]{0,1:T(8,128)(2,1)}) %all-gather.17.cloned.1.call-update) | async-done | bytes 8388624 | tf_op jit(solution)/shard_map/all_gather | solution.py:16
  190.9 7.2 fusion.32
  200.8 22.4 %psum.87 = f32[1024]{0:T(1024)S(1)} all-reduce(f32[1024]{0:T(1024)S(1)} %bitcast.166), channel_id=1, replica_groups=mesh['batch'=4,'row'=16] {'row'}, use_global_device_ids=true, to_apply=%region_3.0 | all-reduce | flops 1024 | bytes 8192 | tf_op jit(solution)/shard_map/psum | solution.py:17
  223.2 35.6 %all-gather.19.cloned.1.call-done = bf16[4096,1024]{0,1:T(8,128)(2,1)} async-done(((bf16[256,1024]{0,1:T(8,128)(2,1)}), bf16[4096,1024]{0,1:T(8,128)(2,1)}) %all-gather.19.cloned.1.call-update) | async-done | bytes 8388624 | tf_op jit(solution)/shard_map/all_gather | solution.py:16
  258.8 7.2 fusion.31
  268.7 22.0 %psum.88 = f32[1024]{0:T(1024)S(1)} all-reduce(f32[1024]{0:T(1024)S(1)} %bitcast.167), channel_id=1, replica_groups=mesh['batch'=4,'row'=16] {'row'}, use_global_device_ids=true, to_apply=%region_4.0 | all-reduce | flops 1024 | bytes 8192 | tf_op jit(solution)/shard_map/psum | solution.py:17
  290.8 34.2 %all-gather.21.cloned.1.call-done = bf16[4096,1024]{0,1:T(8,128)(2,1)} async-done(((bf16[256,1024]{0,1:T(8,128)(2,1)}), bf16[4096,1024]{0,1:T(8,128)(2,1)}) %all-gather.21.cloned.1.call-update) | async-done | bytes 8388624 | tf_op jit(solution)/shard_map/all_gather | solution.py:16
  324.9 7.2 fusion.30
  334.6 21.9 %psum.89 = f32[1024]{0:T(1024)S(1)} all-reduce(f32[1024]{0:T(1024)S(1)} %bitcast.168), channel_id=1, replica_groups=mesh['batch'=4,'row'=16] {'row'}, use_global_device_ids=true, to_apply=%region_5.0 | all-reduce | flops 1024 | bytes 8192 | tf_op jit(solution)/shard_map/psum | solution.py:17
  356.5 35.5 %all-gather.23.cloned.1.call-done = bf16[4096,1024]{0,1:T(8,128)(2,1)} async-done(((bf16[256,1024]{0,1:T(8,128)(2,1)}), bf16[4096,1024]{0,1:T(8,128)(2,1)}) %all-gather.23.cloned.1.call-update) | async-done | bytes 8388624 | tf_op jit(solution)/shard_map/all_gather | solution.py:16
  401.7 21.7 %psum.90 = f32[1024]{0:T(1024)S(1)} all-reduce(f32[1024]{0:T(1024)S(1)} %bitcast.169), channel_id=1, replica_groups=mesh['batch'=4,'row'=16] {'row'}, use_global_device_ids=true, to_apply=%region_6.0 | all-reduce | flops 1024 | bytes 8192 | tf_op jit(solution)/shard_map/psum | solution.py:17
  423.4 35.4 %all-gather.25.cloned.1.call-done = bf16[4096,1024]{0,1:T(8,128)(2,1)} async-done(((bf16[256,1024]{0,1:T(8,128)(2,1)}), bf16[4096,1024]{0,1:T(8,128)(2,1)}) %all-gather.25.cloned.1.call-update) | async-done | bytes 8388624 | tf_op jit(solution)/shard_map/all_gather | solution.py:16
  468.7 21.9 %psum.91 = f32[1024]{0:T(1024)S(1)} all-reduce(f32[1024]{0:T(1024)S(1)} %bitcast.170), channel_id=1, replica_groups=mesh['batch'=4,'row'=16] {'row'}, use_global_device_ids=true, to_apply=%region_7.0 | all-reduce | flops 1024 | bytes 8192 | tf_op jit(solution)/shard_map/psum | solution.py:17
  490.7 35.9 %all-gather.27.cloned.1.call-done = bf16[4096,1024]{0,1:T(8,128)(2,1)} async-done(((bf16[256,1024]{0,1:T(8,128)(2,1)}), bf16[4096,1024]{0,1:T(8,128)(2,1)}) %all-gather.27.cloned.1.call-update) | async-done | bytes 8388624 | tf_op jit(solution)/shard_map/all_gather | solution.py:16
  526.6 7.3 fusion.27
  536.5 21.6 %psum.92 = f32[1024]{0:T(1024)S(1)} all-reduce(f32[1024]{0:T(1024)S(1)} %bitcast.171), channel_id=1, replica_groups=mesh['batch'=4,'row'=16] {'row'}, use_global_device_ids=true, to_apply=%region_8.0 | all-reduce | flops 1024 | bytes 8192 | tf_op jit(solution)/shard_map/psum | solution.py:17
  558.1 35.3 %all-gather.29.cloned.1.call-done = bf16[4096,1024]{0,1:T(8,128)(2,1)} async-done(((bf16[256,1024]{0,1:T(8,128)(2,1)}), bf16[4096,1024]{0,1:T(8,128)(2,1)}) %all-gather.29.cloned.1.call-update) | async-done | bytes 8388624 | tf_op jit(solution)/shard_map/all_gather | solution.py:16
  593.4 7.2 fusion.26
  603.1 22.1 %psum.93 = f32[1024]{0:T(1024)S(1)} all-reduce(f32[1024]{0:T(1024)S(1)} %bitcast.172), channel_id=1, replica_groups=mesh['batch'=4,'row'=16] {'row'}, use_global_device_ids=true, to_apply=%region_9.0 | all-reduce | flops 1024 | bytes 8192 | tf_op jit(solution)/shard_map/psum | solution.py:17
  625.2 35.7 %all-gather.31.cloned.1.call-done = bf16[4096,1024]{0,1:T(8,128)(2,1)} async-done(((bf16[256,1024]{0,1:T(8,128)(2,1)}), bf16[4096,1024]{0,1:T(8,128)(2,1)}) %all-gather.31.cloned.1.call-update) | async-done | bytes 8388624 | tf_op jit(solution)/shard_map/all_gather | solution.py:16
  670.5 22.1 %psum.94 = f32[1024]{0:T(1024)S(1)} all-reduce(f32[1024]{0:T(1024)S(1)} %bitcast.173), channel_id=1, replica_groups=mesh['batch'=4,'row'=16] {'row'}, use_global_device_ids=true, to_apply=%region_10.0 | all-reduce | flops 1024 | bytes 8192 | tf_op jit(solution)/shard_map/psum | solution.py:17
  692.6 35.1 %all-gather.33.cloned.1.call-done = bf16[4096,1024]{0,1:T(8,128)(2,1)} async-done(((bf16[256,1024]{0,1:T(8,128)(2,1)}), bf16[4096,1024]{0,1:T(8,128)(2,1)}) %all-gather.33.cloned.1.call-update) | async-done | bytes 8388624 | tf_op jit(solution)/shard_map/all_gather | solution.py:16
  737.4 22.4 %psum.95 = f32[1024]{0:T(1024)S(1)} all-reduce(f32[1024]{0:T(1024)S(1)} %bitcast.162), channel_id=1, replica_groups=mesh['batch'=4,'row'=16] {'row'}, use_global_device_ids=true, to_apply=%region_11.0 | all-reduce | flops 1024 | bytes 8192 | tf_op jit(solution)/shard_map/psum | solution.py:17
  759.8 35.0 %all-gather.35.cloned.1.call-done = bf16[4096,1024]{0,1:T(8,128)(2,1)} async-done(((bf16[256,1024]{0,1:T(8,128)(2,1)}), bf16[4096,1024]{0,1:T(8,128)(2,1)}) %all-gather.35.cloned.1.call-update) | async-done | bytes 8388624 | tf_op jit(solution)/shard_map/all_gather | solution.py:16
  794.8 7.4 fusion.23
  (63 shorter events, 53.8 us)
Async XLA Ops:
  6.5 57.2 %copy-start = (bf16[256,4096]{1,0:T(8,128)(2,1)S(1)}, bf16[256,4096]{1,0:T(8,128)(2,1)}, u32[]{:S(2)}) copy-start(bf16[256,4096]{1,0:T(8,128)(2,1)} %param.5) | copy-start | bytes 6291460
  6.6 57.2 %all-gather.13.cloned.1.call-start = ((), (), s32[]{:S(2)}) async-start(), calls=%async_computation | async-start | bytes 8912896 | tf_op jit(solution)/shard_map/all_gather | solution.py:16
  8.9 114.0 %all-gather.15.cloned.1.call-start = ((), (), s32[]{:S(2)}) async-start(), calls=%async_computation.1 | async-start | bytes 8912896 | tf_op jit(solution)/shard_map/all_gather | solution.py:16
  39.7 32.8 %copy-start.1 = (f32[256,1024]{1,0:T(8,128)S(1)}, f32[256,1024]{1,0:T(8,128)}, u32[]{:S(2)}) copy-start(f32[256,1024]{1,0:T(8,128)} %param.6) | copy-start | bytes 3145732
  71.3 119.5 %all-gather.17.cloned.1.call-start = ((), (), s32[]{:S(2)}) async-start(), calls=%async_computation.2 | async-start | bytes 8912896 | tf_op jit(solution)/shard_map/all_gather | solution.py:16
  98.1 92.8 %copy-start.2 = (f32[256,1024]{0,1:T(8,128)S(1)}, f32[256,1024]{0,1:T(8,128)}, u32[]{:S(2)}) copy-start(f32[256,1024]{0,1:T(8,128)} %copy.6) | copy-start | bytes 3145732
  130.4 128.5 %all-gather.19.cloned.1.call-start = ((), (), s32[]{:S(2)}) async-start(), calls=%async_computation.3 | async-start | bytes 8912896 | tf_op jit(solution)/shard_map/all_gather | solution.py:16
  198.1 126.9 %all-gather.21.cloned.1.call-start = ((), (), s32[]{:S(2)}) async-start(), calls=%async_computation.4 | async-start | bytes 8912896 | tf_op jit(solution)/shard_map/all_gather | solution.py:16
  266.1 125.9 %all-gather.23.cloned.1.call-start = ((), (), s32[]{:S(2)}) async-start(), calls=%async_computation.5 | async-start | bytes 8912896 | tf_op jit(solution)/shard_map/all_gather | solution.py:16
  332.2 126.6 %all-gather.25.cloned.1.call-start = ((), (), s32[]{:S(2)}) async-start(), calls=%async_computation.6 | async-start | bytes 8912896 | tf_op jit(solution)/shard_map/all_gather | solution.py:16
  399.2 127.4 %all-gather.27.cloned.1.call-start = ((), (), s32[]{:S(2)}) async-start(), calls=%async_computation.7 | async-start | bytes 8912896 | tf_op jit(solution)/shard_map/all_gather | solution.py:16
  466.0 127.4 %all-gather.29.cloned.1.call-start = ((), (), s32[]{:S(2)}) async-start(), calls=%async_computation.8 | async-start | bytes 8912896 | tf_op jit(solution)/shard_map/all_gather | solution.py:16
  533.9 127.0 %all-gather.31.cloned.1.call-start = ((), (), s32[]{:S(2)}) async-start(), calls=%async_computation.9 | async-start | bytes 8912896 | tf_op jit(solution)/shard_map/all_gather | solution.py:16
  600.6 127.1 %all-gather.33.cloned.1.call-start = ((), (), s32[]{:S(2)}) async-start(), calls=%async_computation.10 | async-start | bytes 8912896 | tf_op jit(solution)/shard_map/all_gather | solution.py:16
  668.0 126.8 %all-gather.35.cloned.1.call-start = ((), (), s32[]{:S(2)}) async-start(), calls=%async_computation.11 | async-start | bytes 8912896 | tf_op jit(solution)/shard_map/all_gather | solution.py:16
Sparse Core Ops, SparseCore 0:
  9.0 54.7 all-gather.12
  71.4 51.3 all-gather.14
  130.5 60.3 all-gather.16
  198.2 60.5 all-gather.18
  266.2 58.6 all-gather.20
  332.3 59.6 all-gather.22
  399.3 59.4 all-gather.24
  466.1 60.4 all-gather.26
  534.0 59.2 all-gather.28
  600.7 60.0 all-gather.30
  668.2 59.4 all-gather.32
  735.0 59.8 all-gather.34
where the time goes:
time: 815 us; the launch traced here: 812 us
  waiting for transfers between devices  403 us (49%)
  blocking collectives  269 us (33%)
  matrix products  102 us (13%)
  between operations  28.1 us (3%)
    all_gather x12, waiting for transfers between devices, local_sweeps(): lax.all_gather(rank_rows.astype(jnp.bfloat16), 'row', axis=0, tiled=True)  402 us
    psum x12, blocking collectives, local_sweeps(): lax.psum(jnp.dot(dang_float, rank_rows, preferred_element_type=jnp.float3...  269 us
    dot_general x12, matrix products, local_sweeps(): prod_rows = jnp.dot(mat_rows, gathered, preferred_element_type=jnp.float32)  86.8 us
  transfers between devices with their start and end apart: 12, of which 12 were waited for; matrix products, arithmetic and copies ran while one was open for 2% of the time, Pallas kernels for 0%

commit v1 on v0

v1 whole, which is shorter than its diff:
```python
import functools

import jax
import jax.numpy as jnp
from jax import lax
from jax.experimental import pallas as pl
from jax.experimental.pallas import tpu as pltpu
from jax.sharding import PartitionSpec as P

F32 = jnp.float32
BF16 = jnp.bfloat16


def sweeps_kernel(chips, num_nodes, sweeps,
                  damp_ref, dang_ref, mat_ref, tele_ref, init_ref, out_ref,
                  mat_t, mat_nat, tele_raw, tele_t, init_f32, init_send, init_recv,
                  rank_own, rank_sib, part, mass_send, mass_recv, dang, mass_own, mass_sib, out_stage,
                  ring_send, ring_recv, tele_send, tele_recv, init_ssem, init_rsem, dang_send, dang_recv,
                  mass_ssem, mass_rsem, rank_send, rank_recv, sum_send, sum_recv, out_send, out_recv, load_sem):
    rows = init_ref.shape[0]
    width = init_ref.shape[1] // chips
    half = chips * rows
    num_chunks = 4
    chunk = 2 * half // num_chunks
    me = lax.axis_index("row")
    z = me // 2
    core = lax.rem(me, 2)
    sibling = {"row": me + 1 - 2 * core}

    def chip(offset):
        return lax.rem(z + offset + chips, chips)

    def peer(chip_index):
        return {"row": 2 * chip_index + core}

    def lanes(block, size):
        return pl.ds(pl.multiple_of(block * size, size), size)

    def remote(src, dst, ssem, rsem, device):
        return pltpu.make_async_remote_copy(src_ref=src, dst_ref=dst, send_sem=ssem, recv_sem=rsem,
                                            device_id=device, device_id_type=pl.DeviceIdType.MESH)

    load_mat = pltpu.make_async_copy(mat_ref, mat_nat, load_sem.at[0])
    load_init = pltpu.make_async_copy(init_ref, init_f32, load_sem.at[1])
    load_dang = pltpu.make_async_copy(dang_ref, dang.at[z], load_sem.at[2])
    load_tele = pltpu.make_async_copy(tele_ref.at[:, lanes(z, width)], tele_raw.at[z], load_sem.at[3])
    load_init.start()
    load_dang.start()
    load_mat.start()
    load_tele.start()

    barrier = pltpu.get_barrier_semaphore()
    for offset in range(1, chips):
        pl.semaphore_signal(barrier, inc=1, device_id=peer(chip(offset)), device_id_type=pl.DeviceIdType.MESH)
    pl.semaphore_signal(barrier, inc=1, device_id=sibling, device_id_type=pl.DeviceIdType.MESH)
    pl.semaphore_wait(barrier, chips)

    far_first = sorted(range(1, chips), key=lambda offset: -min(offset, chips - offset))

    def tele_copy(offset):
        return remote(tele_ref.at[:, lanes(chip(offset), width)], tele_raw.at[z],
                      tele_send.at[offset], tele_recv.at[offset], peer(chip(offset)))

    def init_copy(offset):
        return remote(init_send.at[chip(offset)], init_recv.at[z],
                      init_ssem.at[offset], init_rsem.at[offset], peer(chip(offset)))

    def dang_copy(offset):
        return remote(dang.at[z], dang.at[z], dang_send.at[offset], dang_recv.at[offset], peer(chip(offset)))

    def mass_copy(offset):
        return remote(mass_send.at[chip(offset)], mass_recv.at[z],
                      mass_ssem.at[offset], mass_rsem.at[offset], peer(chip(offset)))

    def ring_copy(direction, step, piece):
        sign = 1 - 2 * direction
        slot = mat_t.at[chip(-sign * step), pl.ds(piece * chunk, chunk), :]
        return remote(slot, slot, ring_send.at[direction, step, piece], ring_recv.at[direction, step + 1, piece],
                      peer(chip(sign)))

    def ring_pieces(direction, step):
        if step < chips // 2 - 1:
            return range(num_chunks)
        return range(num_chunks // 2) if direction == 0 else range(num_chunks // 2, num_chunks)

    for offset in far_first:
        tele_copy(offset).start()

    load_dang.wait()
    load_init.wait()
    dang_cols = jnp.transpose(jnp.broadcast_to(dang[z][0:1, :], (width, rows)))
    for j in range(chips):
        tile = init_f32[:, j * width:(j + 1) * width]
        init_send[j] = tile.astype(BF16)
        mass_send[j] = jnp.broadcast_to(jnp.sum(tile * dang_cols, axis=0, keepdims=True), (8, width))
    for offset in far_first:
        init_copy(offset).start()
        mass_copy(offset).start()
        dang_copy(offset).start()

    load_mat.wait()
    for piece in range(num_chunks):
        for k in range(piece * chunk // rows, (piece + 1) * chunk // rows):
            block = 2 * (k % chips) + k // chips
            mat_t[z, k * rows:(k + 1) * rows, :] = jnp.transpose(mat_nat[:, block * rows:(block + 1) * rows])
        for direction in range(2):
            ring_copy(direction, 0, piece).start()

    init_recv[z] = init_send[z]
    mass_recv[z] = mass_send[z]
    for offset in far_first:
        init_copy(offset).wait_recv()
    for j in range(chips):
        rank_own[0, :, j * rows:(j + 1) * rows] = jnp.transpose(init_recv[j])

    def rank_copy(slot, block):
        where = lanes(block, rows)
        return remote(rank_own.at[slot, :, where], rank_sib.at[slot, :, where],
                      rank_send.at[slot], rank_recv.at[slot], sibling)

    def rank_all(slot):
        return remote(rank_own.at[slot], rank_sib.at[slot], rank_send.at[slot], rank_recv.at[slot], sibling)

    def sum_copy(slot):
        return remote(mass_own.at[slot], mass_sib.at[slot], sum_send.at[slot], sum_recv.at[slot], sibling)

    rank_all(0).start()
    for offset in far_first:
        mass_copy(offset).wait_recv()
    mass_row = jnp.sum(mass_recv[...], axis=0)[0:1, :]
    mass_cols = jnp.transpose(jnp.broadcast_to(mass_row, (width, width)))
    first_lane = lax.broadcasted_iota(jnp.int32, (width, width), 1) == 0
    mass_own[0] = jnp.where(first_lane, mass_cols, 0.0)
    sum_copy(0).start()

    for offset in far_first:
        dang_copy(offset).wait_recv()
        tele_copy(offset).wait_recv()
    load_tele.wait()
    for j in range(chips):
        tele_t[j] = jnp.transpose(tele_raw[j])

    def mass_term(slot, factor):
        total = jnp.sum(mass_own[slot] + mass_sib[slot], axis=1, keepdims=True)
        return (factor / num_nodes) * total

    def own_part(slot, block):
        return jnp.dot(rank_own[slot], mat_t[block, pl.ds(pl.multiple_of(core * half, half), half), :],
                       preferred_element_type=F32)

    def sib_part(slot, block):
        return jnp.dot(rank_sib[slot], mat_t[block, pl.ds(pl.multiple_of((1 - core) * half, half), half), :],
                       preferred_element_type=F32)

    def next_rank(prod, block, factor, mass):
        return factor * prod + (1.0 - factor) * tele_t[block] + mass

    def masked(rank, block):
        prod = rank * dang[block][0:1, :]
        total = prod[:, :width]
        for j in range(1, rows // width):
            total = total + prod[:, j * width:(j + 1) * width]
        return total

    rank_all(0).wait()
    sum_copy(0).wait()
    factor0 = damp_ref[0]
    mass0 = mass_term(0, factor0)
    mass_own[1] = jnp.zeros((width, width), F32)

    def first_sweep_block(block):
        prod = own_part(0, block) + sib_part(0, block)
        rank = next_rank(prod, block, factor0, mass0)
        rank_own[1, :, lanes(block, rows)] = rank.astype(BF16)
        mass_own[1] = mass_own[1] + masked(rank, block)
        rank_copy(1, block).start()

    first_sweep_block(z)
    for step in range(1, chips // 2 + 1):
        for piece in range(num_chunks):
            for direction in range(2):
                if piece in ring_pieces(direction, step - 1):
                    ring_copy(direction, step - 1, piece).wait_recv()
                if step < chips // 2 and piece in ring_pieces(direction, step):
                    ring_copy(direction, step, piece).start()
        first_sweep_block(chip(-step))
        if step < chips // 2:
            first_sweep_block(chip(step))
    sum_copy(1).start()

    def sweep(t, carry):
        now = lax.rem(t, 2)
        later = 1 - now
        factor = damp_ref[t]
        for block in range(chips):
            part[block] = own_part(now, block)
        rank_all(now).wait()
        sum_copy(now).wait()
        mass = mass_term(now, factor)
        total = jnp.zeros((width, width), F32)
        for block in range(chips):
            prod = part[block] + sib_part(now, block)
            rank = next_rank(prod, block, factor, mass)
            rank_own[later, :, block * rows:(block + 1) * rows] = rank.astype(BF16)
            total = total + masked(rank, block)
            rank_copy(later, block).start()
        mass_own[later] = total
        sum_copy(later).start()
        return carry

    lax.fori_loop(1, sweeps - 1, sweep, 0)

    last = sweeps - 1
    now = last % 2
    factor = damp_ref[last]
    for block in range(chips):
        part[block] = own_part(now, block)
    rank_all(now).wait()
    sum_copy(now).wait()
    mass = mass_term(now, factor)

    def out_copy(offset):
        return remote(out_stage.at[chip(offset)], out_ref.at[:, lanes(z, width)],
                      out_send.at[offset], out_recv.at[offset], peer(chip(offset)))

    keep = pltpu.make_async_copy(out_stage.at[z], out_ref.at[:, lanes(z, width)], load_sem.at[0])
    for offset in far_first + [0]:
        block = chip(offset)
        prod = part[block] + sib_part(now, block)
        out_stage[block] = jnp.transpose(next_rank(prod, block, factor, mass))
        if offset:
            out_copy(offset).start()
        else:
            keep.start()

    for offset in far_first:
        tele_copy(offset).wait_send()
        init_copy(offset).wait_send()
        mass_copy(offset).wait_send()
        dang_copy(offset).wait_send()
    for step in range(chips // 2):
        for direction in range(2):
            for piece in ring_pieces(direction, step):
                ring_copy(direction, step, piece).wait_send()
    keep.wait()
    for offset in far_first:
        out_copy(offset).wait()


def solution(mesh):
    chips = mesh.shape["row"] // 2
    spec_rows = P(("batch", "row"), None)
    spec_vec = P(("batch", "row"))

    def local_sweeps(mat_rows, tele_rows, dang_rows, damping, start_rows):
        rows, num_nodes = mat_rows.shape
        width = start_rows.shape[1] // chips
        sweeps = damping.shape[0]
        dang_tile = jnp.broadcast_to(dang_rows.astype(F32)[None, :], (8, rows))
        dma = pltpu.SemaphoreType.DMA
        hbm = pl.BlockSpec(memory_space=pl.ANY)
        return pl.pallas_call(
            functools.partial(sweeps_kernel, chips, num_nodes, sweeps),
            out_shape=jax.ShapeDtypeStruct(start_rows.shape, F32),
            in_specs=[pl.BlockSpec(memory_space=pltpu.SMEM), hbm, hbm, hbm, hbm],
            out_specs=hbm,
            scratch_shapes=[
                pltpu.VMEM((chips, num_nodes, rows), BF16),
                pltpu.VMEM((rows, num_nodes), BF16),
                pltpu.VMEM((chips, rows, width), F32),
                pltpu.VMEM((chips, width, rows), F32),
                pltpu.VMEM(start_rows.shape, F32),
                pltpu.VMEM((chips, rows, width), BF16),
                pltpu.VMEM((chips, rows, width), BF16),
                pltpu.VMEM((2, width, chips * rows), BF16),
                pltpu.VMEM((2, width, chips * rows), BF16),
                pltpu.VMEM((chips, width, rows), F32),
                pltpu.VMEM((chips, 8, width), F32),
                pltpu.VMEM((chips, 8, width), F32),
                pltpu.VMEM((chips, 8, rows), F32),
                pltpu.VMEM((2, width, width), F32),
                pltpu.VMEM((2, width, width), F32),
                pltpu.VMEM((chips, rows, width), F32),
                dma((2, chips // 2, 4)), dma((2, chips // 2 + 1, 4)),
                dma((chips,)), dma((chips,)),
                dma((chips,)), dma((chips,)),
                dma((chips,)), dma((chips,)),
                dma((chips,)), dma((chips,)),
                dma((2,)), dma((2,)),
                dma((2,)), dma((2,)),
                dma((chips,)), dma((chips,)),
                dma((4,)),
            ],
            compiler_params=pltpu.CompilerParams(collective_id=0, has_side_effects=True),
        )(damping, dang_tile, mat_rows, tele_rows, start_rows)

    return jax.shard_map(local_sweeps, mesh=mesh, in_specs=(spec_rows, spec_rows, spec_vec, P(None), spec_rows),
                         out_specs=spec_rows, check_vma=False)
```

time: 815 us -> 284 us (0.35)
  waiting for transfers between devices: 403 us -> 0 us
  Pallas kernels: 0 us -> 281 us
  blocking collectives: 269 us -> 0 us
  matrix products: 102 us -> 0 us
  between operations: 28.1 us -> 0.01 us
    all_gather x12 -> x0, waiting for transfers between devices: 402 us -> none  [local_sweeps(): lax.all_gather(rank_rows.astype(jnp.bfloat16), 'row', axis=0, tiled=True)]
    pallas_call x0 -> x1, Pallas kernels: none -> 281 us  [local_sweeps(): pl.pallas_call(functools.partial(sweeps_kernel, chips, num_nodes, sweeps)...]
    psum x12 -> x0, blocking collectives: 269 us -> none  [local_sweeps(): lax.psum(jnp.dot(dang_float, rank_rows, preferred_element_type=jnp.float3...]
    dot_general x24 -> x0, matrix products: 102 us -> none  [the longest x12 86.8 us: local_sweeps(): prod_rows = jnp.dot(mat_rows, gathered, preferred_element_type=jnp.float32)]
  transfers between devices with their start and end apart: 12 -> 0, of which waited for: 12 -> 0; matrix products, arithmetic and copies ran while one was open for 2% -> 0% of each run, Pallas kernels for 0% -> 0%
where the time goes in v1:
time: 284 us
  Pallas kernels  281 us (99%)
  local copies, waits for them, and re-layouts  2.91 us (1%)
    pallas_call x1, Pallas kernels, local_sweeps(): pl.pallas_call(functools.partial(sweeps_kernel, chips, num_nodes, sweeps)...  281 us

profile of v1, /device:TPU:53, one launch (start us, length us, event | category | flops | bytes accessed | tf_op | source)
XLA Modules:
  0.0 284.2 jit_solution(15040868239069488300)
XLA Ops:
  0.0 0.7 convert_element_type.3
  0.7 0.6 broadcast_in_dim.2.dang_ref
  1.3 280.6 %shard_map.55 = f32[256,1024]{1,0:T(8,128)} custom-call(f32[12]{0:T(128)} %damp_ref.1, f32[8,256]{1,0:T(8,128)} %broadcast_in_dim.2.dang_ref, bf16[256,4096]{1,0:T(8,128)(2,1)} %mat_ref.1, f32[256,1024]{1,0:T(8,128)} %tele_ref.1, f32[256,1024]{1,0:T(8,128)} %init_ref.1), custom_call_target="tpu_custom_call" | custom-call | tf_op jit(solution)/shard_map/pallas_call | solution.py:262
  281.9 2.3 copy.7

commit v2 on v1

--- a/solution.py
+++ b/solution.py
@@ -111,11 +111,15 @@
     for offset in far_first:
         init_copy(offset).wait_recv()
     for j in range(chips):
-        rank_own[0, :, j * rows:(j + 1) * rows] = jnp.transpose(init_recv[j])
+        rank_own[0, j] = jnp.transpose(init_recv[j])
 
     def rank_copy(slot, block):
-        where = lanes(block, rows)
-        return remote(rank_own.at[slot, :, where], rank_sib.at[slot, :, where],
+        return remote(rank_own.at[slot, block], rank_sib.at[slot, block],
+                      rank_send.at[slot], rank_recv.at[slot], sibling)
+
+    def rank_some(slot, block, count):
+        where = pl.ds(block, count)
+        return remote(rank_own.at[slot, where], rank_sib.at[slot, where],
                       rank_send.at[slot], rank_recv.at[slot], sibling)
 
     def rank_all(slot):
@@ -144,12 +148,15 @@
         total = jnp.sum(mass_own[slot] + mass_sib[slot], axis=1, keepdims=True)
         return (factor / num_nodes) * total
 
+    def joined(rank, slot):
+        return jnp.concatenate([rank[slot, k] for k in range(chips)], axis=1)
+
     def own_part(slot, block):
-        return jnp.dot(rank_own[slot], mat_t[block, pl.ds(pl.multiple_of(core * half, half), half), :],
+        return jnp.dot(joined(rank_own, slot), mat_t[block, pl.ds(pl.multiple_of(core * half, half), half), :],
                        preferred_element_type=F32)
 
     def sib_part(slot, block):
-        return jnp.dot(rank_sib[slot], mat_t[block, pl.ds(pl.multiple_of((1 - core) * half, half), half), :],
+        return jnp.dot(joined(rank_sib, slot), mat_t[block, pl.ds(pl.multiple_of((1 - core) * half, half), half), :],
                        preferred_element_type=F32)
 
     def next_rank(prod, block, factor, mass):
@@ -171,7 +178,7 @@
     def first_sweep_block(block):
         prod = own_part(0, block) + sib_part(0, block)
         rank = next_rank(prod, block, factor0, mass0)
-        rank_own[1, :, lanes(block, rows)] = rank.astype(BF16)
+        rank_own[1, block] = rank.astype(BF16)
         mass_own[1] = mass_own[1] + masked(rank, block)
         rank_copy(1, block).start()
 
@@ -198,12 +205,20 @@
         sum_copy(now).wait()
         mass = mass_term(now, factor)
         total = jnp.zeros((width, width), F32)
-        for block in range(chips):
-            prod = part[block] + sib_part(now, block)
-            rank = next_rank(prod, block, factor, mass)
-            rank_own[later, :, block * rows:(block + 1) * rows] = rank.astype(BF16)
-            total = total + masked(rank, block)
-            rank_copy(later, block).start()
+        prod = None
+        for ahead in range(chips + 1):
+            done = prod
+            if ahead < chips:
+                prod = part[ahead] + sib_part(now, ahead)
+            if ahead:
+                block = ahead - 1
+                rank = next_rank(done, block, factor, mass)
+                rank_own[later, block] = rank.astype(BF16)
+                total = total + masked(rank, block)
+                if block == 5:
+                    rank_some(later, 0, 6).start()
+                if block == 7:
+                    rank_some(later, 6, 2).start()
         mass_own[later] = total
         sum_copy(later).start()
         return carry
@@ -272,8 +287,8 @@
                 pltpu.VMEM(start_rows.shape, F32),
                 pltpu.VMEM((chips, rows, width), BF16),
                 pltpu.VMEM((chips, rows, width), BF16),
-                pltpu.VMEM((2, width, chips * rows), BF16),
-                pltpu.VMEM((2, width, chips * rows), BF16),
+                pltpu.VMEM((2, chips, width, rows), BF16),
+                pltpu.VMEM((2, chips, width, rows), BF16),
                 pltpu.VMEM((chips, width, rows), F32),
                 pltpu.VMEM((chips, 8, width), F32),
                 pltpu.VMEM((chips, 8, width), F32),

time: 284 us -> 267 us (0.940)
  Pallas kernels: 281 us -> 264 us
    pallas_call x1, Pallas kernels: 281 us -> 264 us  [local_sweeps(): pl.pallas_call(functools.partial(sweeps_kernel, chips, num_nodes, sweeps)...]
where the time goes in v2:
time: 267 us
  Pallas kernels  264 us (99%)
  local copies, waits for them, and re-layouts  2.91 us (1%)
    pallas_call x1, Pallas kernels, local_sweeps(): pl.pallas_call(functools.partial(sweeps_kernel, chips, num_nodes, sweeps)...  264 us

profile of v2, /device:TPU:53, one launch (start us, length us, event | category | flops | bytes accessed | tf_op | source)
XLA Modules:
  0.0 267.3 jit_solution(5124847484272844479)
XLA Ops:
  0.0 0.7 convert_element_type.3
  0.7 0.6 broadcast_in_dim.2.dang_ref
  1.3 263.7 %shard_map.55 = f32[256,1024]{1,0:T(8,128)} custom-call(f32[12]{0:T(128)} %damp_ref.1, f32[8,256]{1,0:T(8,128)} %broadcast_in_dim.2.dang_ref, bf16[256,4096]{1,0:T(8,128)(2,1)} %mat_ref.1, f32[256,1024]{1,0:T(8,128)} %tele_ref.1, f32[256,1024]{1,0:T(8,128)} %init_ref.1), custom_call_target="tpu_custom_call" | custom-call | tf_op jit(solution)/shard_map/pallas_call | solution.py:277
  265.0 2.3 copy.7
